TPU v7x, 32 devices: a whole 2x2x4 slice. The times are simulated.
32 devices in a mesh: grp: 2 (over core), dev: 16 (over z, y, x).
Axes of the slice: x: 2, y: 2, z: 4, core: 2. Of those that a mesh axis runs over, the one named last changes fastest.
Arguments:
- accum: float32 [4096, 24, 128], P(('grp', 'dev')), may hold values from -48 to 48
- step_count: int32 [24], replicated, may hold values from 1 to 12
- stretch_slot: int32 [4096], replicated, may hold values from 0 to 4095, as said below
- span_length: int32 [32], replicated, may hold values from 1 to 256, 4096 in all
- wet_mask: int32 [8192], P(('grp', 'dev')), may hold values 0 or 1
Outputs:
- ocean_flux: float32 [8192, 24, 128], P(('grp', 'dev'))
Inputs may be any that keep to these rules, and one draw needn't show every extreme that they name: `stretch_slot`: A permutation of the slots; any 32 consecutive row blocks lie on 32 different atmosphere devices (slot // 128). `span_length`: sums to 4096; some ocean device owns exactly 256 blocks. `wet_mask`: entries of slots beyond an ocean device's span are ignored.
All inputs are finite; a program needn't handle non-finite values.
Results may differ from a plain program's by a relative error of at most 0.000071.
Values sent between devices are 32-bit elements; how exact they have to be, the bound alone decides.
A program may use at most 64 MiB of HBM per device.

v0:
```python
import jax
import jax.numpy as jnp
from jax import lax
from jax.sharding import PartitionSpec as P


def passed_along(value, axis, steps):
    count = lax.axis_size(axis)
    initial, last = (max(0, -steps), min(count, count - steps))
    return lax.ppermute(value, axis, [(source, source + steps) for source in range(initial, last)])


def select_rows(picks, table):
    return jnp.dot(
        picks, table, precision=lax.Precision.HIGHEST, preferred_element_type=jnp.float32
    )


def on_device(accum, step_count, stretch_slot, span_length, wet_mask):
    devices = lax.axis_size(("grp", "dev"))
    my_index = lax.axis_index(("grp", "dev"))
    blocks_dev = accum.shape[0]
    fields = accum.shape[1]
    cells = accum.shape[2]
    capacity = wet_mask.shape[0]
    pair_most = capacity // devices
    all_blocks = stretch_slot.shape[0]
    span_end = jnp.cumsum(span_length)
    span_start = span_end - span_length
    all_ids = jnp.arange(all_blocks, dtype=jnp.int32)
    local_ids = jnp.arange(blocks_dev, dtype=jnp.int32)
    mine = stretch_slot[None, :] == (my_index * blocks_dev + local_ids)[:, None]
    my_global = jnp.sum(jnp.where(mine, all_ids[None, :], 0), axis=1)
    owner = jnp.sum((span_end[None, :] <= my_global[:, None]).astype(jnp.int32), axis=1)
    same_owner = owner[:, None] == owner[None, :]
    earlier = my_global[None, :] < my_global[:, None]
    order_in = jnp.sum((same_owner & earlier).astype(jnp.int32), axis=1)
    position = owner * pair_most + order_in
    buffer_ids = jnp.arange(devices * pair_most, dtype=jnp.int32)
    send_picks = (position[None, :] == buffer_ids[:, None]).astype(jnp.float32)
    counts = step_count.astype(jnp.float32)
    normal = (accum / counts[None, :, None]).reshape(blocks_dev, fields * cells)
    sendbuf = select_rows(send_picks, normal).reshape(devices, pair_most, fields, cells)
    received = lax.all_to_all(sendbuf, ("grp", "dev"), split_axis=0, concat_axis=0, tiled=True)
    received = received.reshape(devices * pair_most, fields * cells)
    length = span_length[my_index]
    start = span_start[my_index]
    slots = jnp.arange(capacity, dtype=jnp.int32)
    valid = slots < length
    global_ids = jnp.minimum(start + slots, all_blocks - 1)
    sender = stretch_slot[global_ids] // blocks_dev
    same_sender = (sender[:, None] == sender[None, :]) & valid[None, :]
    lower = slots[None, :] < slots[:, None]
    rank_in = jnp.sum((same_sender & lower).astype(jnp.int32), axis=1)
    place_ids = sender * pair_most + rank_in
    place_picks = (place_ids[:, None] == buffer_ids[None, :]).astype(jnp.float32)
    placed = select_rows(place_picks, received).reshape(capacity, fields, cells)
    wet = (valid & (wet_mask == 1)).astype(jnp.float32)
    masked = placed * wet[:, None, None]
    last_cells = masked[:, :, cells - 1]
    first_cells = masked[:, :, 0]
    last_cell = lax.dynamic_index_in_dim(last_cells, length - 1, 0, keepdims=False)
    first_cell = first_cells[0]
    left_in = passed_along(last_cell, ("grp", "dev"), 1)
    right_in = passed_along(first_cell, ("grp", "dev"), -1)
    before_col = jnp.concatenate([left_in[None, :], last_cells[:-1]], axis=0)
    after_col = jnp.concatenate([first_cells[1:], jnp.zeros((1, fields), jnp.float32)], axis=0)
    after_col = jnp.where((slots == length - 1)[:, None], right_in[None, :], after_col)
    cell_ids = jnp.arange(cells, dtype=jnp.int32)
    distance = jnp.abs(cell_ids[:, None] - cell_ids[None, :])
    stencil = jnp.where(distance == 0, 0.5, jnp.where(distance == 1, 0.25, 0.0)).astype(jnp.float32)
    inner = jnp.dot(
        masked.reshape(capacity * fields, cells),
        stencil,
        precision=lax.Precision.HIGHEST,
        preferred_element_type=jnp.float32,
    ).reshape(capacity, fields, cells)
    first_hot = (cell_ids == 0).astype(jnp.float32)
    last_hot = (cell_ids == cells - 1).astype(jnp.float32)
    edges_added = (
        0.25 * before_col[:, :, None] * first_hot[None, None, :]
        + 0.25 * after_col[:, :, None] * last_hot[None, None, :]
    )
    smoothed = (inner + edges_added) * wet[:, None, None]
    return smoothed


def solution(mesh):
    return jax.shard_map(
        on_device,
        mesh=mesh,
        in_specs=(P(("grp", "dev"), None, None), P(), P(), P(), P(("grp", "dev"))),
        out_specs=P(("grp", "dev"), None, None),
        check_vma=False,
    )
```

profile of v0, /device:TPU:1, one launch (start us, length us, event | category | flops | bytes accessed | tf_op | source)
XLA Modules:
  0.0 114.0 jit_solution(1477209370959415454)
XLA Ops:
  0.0 0.7 convert_element_type.34
  0.7 0.7 copy.21
  1.4 0.1 reduce-window.8
  1.5 0.1 reduce
  1.6 1.1 select_reduce_fusion
  2.7 0.1 convert_reduce_fusion.2
  2.8 0.2 convert_reduce_fusion.1
  3.0 1.6 %broadcast_divide_fusion = f32[128,24,128]{2,1,0:T(8,128)S(1)} fusion(f32[128,24,128]{2,1,0:T(8,128)} %param.5, f32[24]{0:T(128)S(1)} %convert_element_type.34), kind=kLoop, calls=%fused_computation.5 | loop fusion | flops 393216 | bytes 3145824 | tf_op jit(solution)/shard_map/div | solution.py:42
  4.6 0.3 copy.38
  4.9 0.5 copy.22
  5.4 3.1 %fusion.4 = f32[32,8,24,128]{3,1,2,0:T(8,128)} fusion(f32[24,128,128,1]{2,1,0,3:T(8,128)S(1)} %bitcast.43, s32[32,8]{1,0:T(8,128)S(1)} %multiply_add_fusion, s32[128]{0:T(128)S(1)} %multiply_add_fusion.2), kind=kOutput, calls=%fused_computation.12 | convolution fusion | flops 1207992320 | bytes 4720128 | tf_op jit(solution)/shard_map/dot_general | solution.py:14
  8.5 0.0 copy-start.2
  8.5 0.0 copy-start
  8.5 0.0 copy-start.1
  8.5 7.1 %all-to-all-start = ((f32[32,8,24,128]{3,1,2,0:T(8,128)}), f32[32,8,24,128]{3,1,2,0:T(8,128)S(1)}, u32[]{:S(2)}, u32[]{:S(2)}) async-start(f32[32,8,24,128]{3,1,2,0:T(8,128)} %fusion.4), calls=%async_computation | async-start | bytes 6291456 | tf_op jit(solution)/shard_map/all_to_all | solution.py:44
  15.6 0.0 copy-done.2
  15.6 0.7 dynamic_slice.11
  17.6 0.6 dynamic_slice.10
  18.2 0.6 compare_select_fusion
  18.8 0.0 copy-done
  18.8 1.7 %gather_fusion = s32[256]{0:T(256)S(1)} fusion(s32[4096]{0:T(1024)S(1)} %copy-done, s32[1024]{0:T(1024)S(1)} %pad_clamp_fusion), kind=kCustom, calls=%fused_computation | custom fusion | bytes 3072 | tf_op jit(solution)/shard_map/gather | solution.py:51
  20.6 0.0 copy-done.1
  20.6 0.7 and_convert_fusion
  21.3 0.2 convert_reduce_fusion
  21.5 66.5 %all-to-all-done = f32[32,8,24,128]{3,1,2,0:T(8,128)S(1)} async-done(((f32[32,8,24,128]{3,1,2,0:T(8,128)}), f32[32,8,24,128]{3,1,2,0:T(8,128)S(1)}, u32[]{:S(2)}, u32[]{:S(2)}) %all-to-all-start) | async-done | bytes 3145760 | tf_op jit(solution)/shard_map/all_to_all | solution.py:44
  88.0 2.4 %copy.23 = f32[3072,256]{1,0:T(8,128)} copy(f32[3072,256]{0,1:T(8,128)S(1)} %bitcast.41) | data formatting | bytes 6291456 | tf_op jit(solution)/shard_map/dot_general | solution.py:14
  90.3 3.5 %convolution_multiply_fusion = f32[256,24,128]{0,2,1:T(8,128)S(1)} fusion(f32[24,128,256]{2,1,0:T(8,128)} %bitcast.42, f32[256]{0:T(256)S(1)} %get-tuple-element.7, s32[256]{0:T(256)S(1)} %multiply_add_fusion.1), kind=kOutput, calls=%fused_computation.3 | convolution fusion | flops 2416771072 | bytes 6293504 | tf_op jit(solution)/shard_map/dot_general | solution.py:14
  93.9 0.3 slice_reduce_fusion
  94.2 0.1 fusion.29
  94.3 1.9 %collective-permute-start.1 = (f32[24]{0:T(128)S(1)}, f32[24]{0:T(128)S(1)}, u32[]{:S(2)}, u32[]{:S(2)}) collective-permute-start(f32[24]{0:T(128)S(1)} %slice_reduce_fusion), channel_id=1, source_target_pairs={{1,0},{2,1},{3,2},{4,3},{5,4},{6,5},{7,6},{8,7},{9,8},{10,9},{11,1... | collective-permute-start | bytes 296 | tf_op jit(solution)/shard_map/ppermute | solution.py:10
  96.2 0.4 dynamic-slice_reduce_fusion
  96.6 3.4 %collective-permute-start = (f32[24]{0:T(128)S(1)}, f32[24]{0:T(128)S(1)}, u32[]{:S(2)}, u32[]{:S(2)}) collective-permute-start(f32[24]{0:T(128)S(1)} %dynamic-slice_reduce_fusion), channel_id=1, source_target_pairs={{0,1},{1,2},{2,3},{3,4},{4,5},{5,6},{6,7},{7,8},{8,9},{9,10},{10,1... | collective-permute-start | bytes 296 | tf_op jit(solution)/shard_map/ppermute | solution.py:10
  100.0 5.1 %collective-permute-done = f32[24]{0:T(128)S(1)} collective-permute-done((f32[24]{0:T(128)S(1)}, f32[24]{0:T(128)S(1)}, u32[]{:S(2)}, u32[]{:S(2)}) %collective-permute-start) | collective-permute-done | bytes 128 | tf_op jit(solution)/shard_map/ppermute | solution.py:10
  105.1 0.1 copy.26
  105.2 0.1 maximum_multiply_fusion
  105.3 0.0 collective-permute-done.1
  105.3 0.1 select_multiply_fusion
  105.3 5.1 %add_multiply_fusion = f32[256,24,128]{0,2,1:T(8,128)} fusion(f32[128]{0:T(128)S(1)} %get-tuple-element.9, f32[256,24]{0,1:T(8,128)S(1)} %select_multiply_fusion, f32[128]{0:T(128)S(1)} %get-tuple-element.10, f32[256,24]{0,1:T(8,128)S(1)} %maximum_multiply_fusion, f32[256]{0:T(256)S(1)} %get-tuple-element.7, f32[256,24,128]{0,2,1:T(8,128)S(1)} %convolution_multiply_fusion), kind=kOutput, calls=%fused_computation.1 | convolution fusion | flops 1211990016 | bytes 6342656 | tf_op jit(solution)/shard_map/dot_general | solution.py:72
  110.4 3.5 %copy.28 = f32[256,24,128]{2,1,0:T(8,128)} copy(f32[256,24,128]{0,2,1:T(8,128)} %add_multiply_fusion) | data formatting | bytes 6291456 | tf_op jit(solution)/shard_map/mul | solution.py:84
  (12 shorter events, 0.1 us)
Async XLA Ops:
  8.5 7.1 %copy-start.2 = (s32[32]{0:T(128)S(1)}, s32[32]{0:T(128)}, u32[]{:S(2)}) copy-start(s32[32]{0:T(128)} %param.8) | copy-start | bytes 388
  8.5 10.3 %copy-start = (s32[4096]{0:T(1024)S(1)}, s32[4096]{0:T(1024)}, u32[]{:S(2)}) copy-start(s32[4096]{0:T(1024)} %param.7) | copy-start | bytes 49156
  8.5 12.1 %copy-start.1 = (s32[256]{0:T(256)S(1)}, s32[256]{0:T(256)}, u32[]{:S(2)}) copy-start(s32[256]{0:T(256)} %param.9) | copy-start | bytes 3076
  8.5 79.5 %all-to-all-start = ((f32[32,8,24,128]{3,1,2,0:T(8,128)}), f32[32,8,24,128]{3,1,2,0:T(8,128)S(1)}, u32[]{:S(2)}, u32[]{:S(2)}) async-start(f32[32,8,24,128]{3,1,2,0:T(8,128)} %fusion.4), calls=%async_computation | async-start | bytes 6291456 | tf_op jit(solution)/shard_map/all_to_all | solution.py:44
  94.3 11.0 %collective-permute-start.1 = (f32[24]{0:T(128)S(1)}, f32[24]{0:T(128)S(1)}, u32[]{:S(2)}, u32[]{:S(2)}) collective-permute-start(f32[24]{0:T(128)S(1)} %slice_reduce_fusion), channel_id=1, source_target_pairs={{1,0},{2,1},{3,2},{4,3},{5,4},{6,5},{7,6},{8,7},{9,8},{10,9},{11,1... | collective-permute-start | bytes 296 | tf_op jit(solution)/shard_map/ppermute | solution.py:10
  96.6 8.5 %collective-permute-start = (f32[24]{0:T(128)S(1)}, f32[24]{0:T(128)S(1)}, u32[]{:S(2)}, u32[]{:S(2)}) collective-permute-start(f32[24]{0:T(128)S(1)} %dynamic-slice_reduce_fusion), channel_id=1, source_target_pairs={{0,1},{1,2},{2,3},{3,4},{4,5},{5,6},{6,7},{7,8},{8,9},{9,10},{10,1... | collective-permute-start | bytes 296 | tf_op jit(solution)/shard_map/ppermute | solution.py:10
where the time goes:
time: 114 us
  waiting for transfers between devices  71.6 us (63%)
  starting transfers between devices  12.4 us (11%)
  matrix products  11.7 us (10%)
  local copies, waits for them, and re-layouts  11.2 us (10%)
  other arithmetic  5.48 us (5%)
  between operations  1.59 us (1%)
    all_to_all x1, waiting for transfers between devices, on_device(): lax.all_to_all(sendbuf, ('grp', 'dev'), split_axis=0, concat_axis=0, tile...  66.5 us
    all_to_all x1, starting transfers between devices, on_device(): lax.all_to_all(sendbuf, ('grp', 'dev'), split_axis=0, concat_axis=0, tile...  7.08 us
    dot_general x2, matrix products, select_rows(): jnp.dot(picks, table, precision=lax.Precision.HIGHEST, preferred_element_...  6.65 us
    ppermute x2, starting transfers between devices, passed_along(): lax.ppermute(value, axis, [(source, source + steps) for source in range(i...  5.28 us
    ppermute x2, waiting for transfers between devices, passed_along(): lax.ppermute(value, axis, [(source, source + steps) for source in range(i...  5.09 us
    dot_general x1, matrix products, on_device(): jnp.dot(masked.reshape(capacity * fields, cells), stencil, precision=lax....  5.09 us
    mul x1, local copies, waits for them, and re-layouts, on_device(): smoothed = (inner + edges_added) * wet[:, None, None]  3.54 us
    dot_general x2, local copies, waits for them, and re-layouts, select_rows(): jnp.dot(picks, table, precision=lax.Precision.HIGHEST, preferred_element_...  2.81 us
  transfers between devices with their start and end apart: 3, of which 2 were waited for; matrix products, arithmetic and copies ran while one was open for 4% of the time, Pallas kernels for 0%

commit v1 on v0

v1 whole, which is shorter than its diff:
```python
import functools
import jax
import jax.numpy as jnp
from jax import lax
from jax.experimental import pallas as pl
from jax.experimental.pallas import tpu as pltpu
from jax.sharding import PartitionSpec as P

MESH = pl.DeviceIdType.MESH


def exchange_kernel(
    sizes, stretch, spans, wet, accum, received, halo,
    starts, packed, landed, edge_out, edge_in, send_sem, recv_sem, out_sem, edge_send, edge_recv, edge_copy,
):
    groups, chips, layers, pair_most, blocks_dev, all_blocks = sizes
    devices = groups * chips
    plane = chips // layers
    grp = lax.axis_index("grp")
    dev = lax.axis_index("dev")
    me = grp * chips + dev
    layer, place = dev // plane, dev % plane

    def at(index):
        return (index // chips, index % chips)

    barrier = pltpu.get_barrier_semaphore()

    @pl.loop(1, devices)
    def _(step):
        pl.semaphore_signal(barrier, inc=1, device_id=at((me + step) % devices), device_id_type=MESH)

    def prefix(owner, total):
        starts[owner] = total
        return total + spans[owner]

    lax.fori_loop(0, devices, prefix, jnp.int32(0))

    def find(block, found):
        return jnp.where(stretch[block] // blocks_dev == me, block, found)

    phase = lax.fori_loop(0, devices, find, jnp.int32(0), unroll=8)

    def partner(turn, rest):
        there = ((layer + turn) % layers) * plane + (place + rest % plane) % plane
        return ((grp + rest // plane) % groups) * chips + there

    def pack(owner, target, base):
        start = starts[owner]
        first = start + lax.rem(phase - start + all_blocks * devices, devices)
        for rank in range(pair_most):
            block = jnp.minimum(first + rank * devices, all_blocks - 1)
            slot = lax.rem(stretch[block], blocks_dev)
            target[base + rank] = accum[slot]

    def send_copy(other):
        return pltpu.make_async_remote_copy(
            src_ref=packed.at[pl.ds(other * pair_most, pair_most)],
            dst_ref=landed.at[pl.ds(me * pair_most, pair_most)],
            send_sem=send_sem.at[other],
            recv_sem=recv_sem.at[me],
            device_id=at(other),
            device_id_type=MESH,
        )

    def out_copy(other):
        return pltpu.make_async_copy(
            landed.at[pl.ds(other * pair_most, pair_most)],
            received.at[pl.ds(other * pair_most, pair_most)],
            out_sem.at[other],
        )

    turns = [layers // 2] + [t for t in range(1, layers) if t != layers // 2]
    if layers > 1:
        turns = turns + [0]
    else:
        turns = [0]
    rests = groups * plane
    for number, turn in enumerate(turns):
        low = 1 if turn == 0 else 0

        @pl.loop(low, rests)
        def _(rest):
            other = partner(turn, rest)
            pack(other, packed, other * pair_most)

        if number == 0:
            pl.semaphore_wait(barrier, devices - 1)

        @pl.loop(low, rests)
        def _(rest):
            send_copy(partner(turn, rest)).start()

    pack(me, landed, me * pair_most)

    for turn in reversed(turns):
        low = 1 if turn == 0 else 0

        @pl.loop(low, rests)
        def _(rest):
            other = partner(turn, rest)
            pltpu.make_async_remote_copy(
                src_ref=packed.at[pl.ds(other * pair_most, pair_most)],
                dst_ref=landed.at[pl.ds(other * pair_most, pair_most)],
                send_sem=send_sem.at[other],
                recv_sem=recv_sem.at[other],
                device_id=at(other),
                device_id_type=MESH,
            ).wait_recv()
            out_copy(other).start()

    out_copy(me).start()

    start = starts[me]
    length = spans[me]
    first_from = stretch[start] // blocks_dev
    last = jnp.maximum(length - 1, 0)
    last_from = stretch[start + last] // blocks_dev
    edge_out[0] = landed[last_from * pair_most + last // devices] * (
        wet[last] == 1
    ).astype(jnp.float32)
    edge_out[1] = landed[first_from * pair_most] * (wet[0] == 1).astype(jnp.float32)
    copies = []
    for side, shift in ((0, 1), (1, devices - 1)):
        copies.append(
            pltpu.make_async_remote_copy(
                src_ref=edge_out.at[side],
                dst_ref=edge_in.at[side],
                send_sem=edge_send.at[side],
                recv_sem=edge_recv.at[side],
                device_id=at((me + shift) % devices),
                device_id_type=MESH,
            )
        )
    for copy in copies:
        copy.start()

    @pl.loop(1, devices)
    def _(step):
        send_copy((me + step) % devices).wait_send()

    @pl.loop(0, devices)
    def _(other):
        out_copy(other).wait()

    for copy in copies:
        copy.wait()
    final = pltpu.make_async_copy(edge_in, halo, edge_copy)
    final.start()
    final.wait()


def filter_kernel(sizes, chunk, stretch, spans, wet, received, halo, recips, out, origin):
    groups, chips, pair_most, blocks_dev, all_blocks = sizes
    devices = groups * chips
    me = lax.axis_index("grp") * chips + lax.axis_index("dev")
    step = pl.program_id(0)

    @pl.when(step == 0)
    def _():
        origin[0] = lax.fori_loop(
            0, devices, lambda o, s: s + jnp.where(o < me, spans[o], 0), jnp.int32(0), unroll=8
        )

    start = origin[0]
    length = spans[me]
    capacity = wet.shape[0]
    base = step * chunk
    recip = recips[...]
    fields, cells = recip.shape
    lane = lax.broadcasted_iota(jnp.int32, (fields, cells), 1)
    at_first, at_last = lane == 0, lane == cells - 1
    left = halo[0] * recip * jnp.where(me > 0, 1.0, 0.0)
    right = halo[1] * recip * jnp.where(me < devices - 1, 1.0, 0.0)

    def wet_of(slot):
        bit = wet[jnp.clip(slot, 0, capacity - 1)] == 1
        return jnp.where(bit & (slot < length), 1.0, 0.0).astype(jnp.float32)

    def block_of(slot):
        slot = jnp.clip(slot, 0, capacity - 1)
        block = jnp.minimum(start + slot, all_blocks - 1)
        row = (stretch[block] // blocks_dev) * pair_most + slot // devices
        return received[row] * (recip * wet_of(slot))

    before = jnp.where(base == 0, left, block_of(base - 1))
    here = block_of(base)

    def one(offset, carry):
        before, here = carry
        slot = base + offset
        after = jnp.where(slot + 1 == length, right, block_of(slot + 1))
        low = pltpu.roll(jnp.where(at_last, before, here), 1, 1)
        high = pltpu.roll(jnp.where(at_first, after, here), cells - 1, 1)
        out[offset] = (0.25 * low + 0.5 * here + 0.25 * high) * wet_of(slot)
        return here, after

    lax.fori_loop(0, chunk, one, (before, here), unroll=8)


def on_device(accum, step_count, stretch_slot, span_length, wet_mask):
    groups, chips = lax.axis_size("grp"), lax.axis_size("dev")
    devices = groups * chips
    blocks_dev, fields, cells = accum.shape
    capacity = wet_mask.shape[0]
    pair_most = capacity // devices
    all_blocks = stretch_slot.shape[0]
    layers = 4 if chips % 4 == 0 else 1
    smem = pl.BlockSpec(memory_space=pltpu.SMEM)
    vmem = pl.BlockSpec(memory_space=pltpu.VMEM)
    hbm = pl.BlockSpec(memory_space=pl.ANY)
    block = (fields, cells)
    f32 = jnp.float32
    sems = pltpu.SemaphoreType.DMA
    received, halo = pl.pallas_call(
        functools.partial(
            exchange_kernel, (groups, chips, layers, pair_most, blocks_dev, all_blocks)
        ),
        out_shape=(
            jax.ShapeDtypeStruct((capacity, *block), f32),
            jax.ShapeDtypeStruct((2, *block), f32),
        ),
        in_specs=[smem, smem, smem, vmem],
        out_specs=(hbm, hbm),
        scratch_shapes=[
            pltpu.SMEM((devices,), jnp.int32),
            pltpu.VMEM((capacity, *block), f32),
            pltpu.VMEM((capacity, *block), f32),
            pltpu.VMEM((2, *block), f32),
            pltpu.VMEM((2, *block), f32),
            sems((devices,)),
            sems((devices,)),
            sems((devices,)),
            sems((2,)),
            sems((2,)),
            sems,
        ],
        compiler_params=pltpu.CompilerParams(collective_id=0, has_side_effects=True),
    )(stretch_slot, span_length, wet_mask, accum)
    recips = jnp.broadcast_to((1.0 / step_count.astype(f32))[:, None], block)
    chunk = 32 if capacity % 32 == 0 else capacity
    return pl.pallas_call(
        functools.partial(
            filter_kernel, (groups, chips, pair_most, blocks_dev, all_blocks), chunk
        ),
        grid=(capacity // chunk,),
        out_shape=jax.ShapeDtypeStruct((capacity, *block), f32),
        in_specs=[smem, smem, smem, vmem, vmem, vmem],
        out_specs=pl.BlockSpec((chunk, *block), lambda step: (step, 0, 0)),
        scratch_shapes=[pltpu.SMEM((1,), jnp.int32)],
    )(stretch_slot, span_length, wet_mask, received, halo, recips)


def solution(mesh):
    return jax.shard_map(
        on_device,
        mesh=mesh,
        in_specs=(P(("grp", "dev"), None, None), P(), P(), P(), P(("grp", "dev"))),
        out_specs=P(("grp", "dev"), None, None),
        check_vma=False,
    )
```

time: 114 us -> 92 us (0.81)
  the two profiles are of different devices: /device:TPU:1 before, /device:TPU:16 now
where the time goes in v1:
time: 92 us; the launch traced here: 91.9 us
  Pallas kernels  90.5 us (98%)
    pallas_call x1, Pallas kernels, on_device(): pl.pallas_call(functools.partial(exchange_kernel, (groups, chips, layers,...  80.5 us
    pallas_call x1, Pallas kernels, on_device(): pl.pallas_call(functools.partial(filter_kernel, (groups, chips, pair_most...  10.1 us

profile of v1, /device:TPU:16, one launch (start us, length us, event | category | flops | bytes accessed | tf_op | source)
XLA Modules:
  0.0 91.9 jit_solution(9024204235211129810)
XLA Ops:
  0.0 0.7 convert_divide_fusion
  0.7 0.7 broadcast_in_dim.2.recips
  1.3 80.5 %shard_map.55 = (f32[256,24,128]{2,1,0:T(8,128)}, f32[2,24,128]{2,1,0:T(8,128)}) custom-call(s32[4096]{0:T(1024)} %stretch.3, s32[32]{0:T(128)} %spans.3, s32[256]{0:T(256)} %wet.3, f32[128,24,128]{2,1,0:T(8,128)} %accum.1), custom_call_target="tpu_custom_call" | custom-call | tf_op jit(solution)/shard_map/pallas_call | solution.py:215
  81.8 10.1 %shard_map.56 = f32[256,24,128]{2,1,0:T(8,128)} custom-call(s32[4096]{0:T(1024)} %stretch.3, s32[32]{0:T(128)} %spans.3, s32[256]{0:T(256)} %wet.3, f32[256,24,128]{2,1,0:T(8,128)} %get-tuple-element.7.received, f32[2,24,128]{2,1,0:T(8,128)} %get-tuple-element.8.halo, f32[24,128]{1,0:T(8,128)} %broadcast_in_dim.2.recips), custom_call_target="tpu_custom_call" | custom-call | tf_op jit(solution)/shard_map/pallas_call | solution.py:242
